TPU v7x, 32 devices: a whole 2x2x4 slice. The times are simulated.
32 devices in a mesh: px: 4 (over z), py: 4 (over y, x), pz: 2 (over core).
Axes of the slice: x: 2, y: 2, z: 4, core: 2. Of those that a mesh axis runs over, the one named last changes fastest.
Arguments:
- right_side: float32 [16, 64, 256], P('px', 'py', 'pz'), may hold values from -160 to 160
- start_guess: float32 [16, 64, 256], P('px', 'py', 'pz'), may hold values from -4 to 4
- conductivity: float32 [16, 64, 256], P('px', 'py', 'pz'), may hold values from 0.05 to 0.4
- recycled: float32 [16, 16, 64, 256], P(None, 'px', 'py', 'pz'), may hold values from -6 to 6
Outputs:
- solution: float32 [16, 64, 256], P('px', 'py', 'pz')
- residual: float32 [16, 64, 256], P('px', 'py', 'pz')
- hessenberg: float32 [9, 8], replicated
All inputs are finite; a program needn't handle non-finite values.
Results may differ from a plain program's by a relative error of at most 0.03.
Values sent between devices are 32-bit elements; how exact they have to be, the bound alone decides.
A program may use at most 128 MiB of HBM per device.

v0:
```python
import jax
import jax.numpy as jnp
from jax import lax
from jax.sharding import PartitionSpec as P

STEPS = 8
highest = lax.Precision.HIGHEST
edge_weight = 0.25 ** (1.0 / 3.0)
middle_weight = 2.0 * edge_weight
shift_value = 0.4


def padded_2(array, sides, width):
    for axis, dim in sides:
        peers, length = (lax.axis_size(axis), array.shape[dim])
        up = [(i, (i + 1) % peers) for i in range(peers - 1)]
        down = [(j, i) for i, j in up]
        last = lax.slice_in_dim(array, length - width, length, axis=dim)
        leading = lax.slice_in_dim(array, 0, width, axis=dim)
        before = lax.ppermute(last, axis, up)
        after = lax.ppermute(leading, axis, down)
        array = jnp.concatenate([before, array, after], axis=dim)
    return array


def stencil_sum(padded):
    along_z = edge_weight * (padded[..., :-2] + padded[..., 2:]) + middle_weight * padded[..., 1:-1]
    along_y = (
        edge_weight * (along_z[..., :-2, :] + along_z[..., 2:, :])
        + middle_weight * along_z[..., 1:-1, :]
    )
    along_x = (
        edge_weight * (along_y[..., :-2, :, :] + along_y[..., 2:, :, :])
        + middle_weight * along_y[..., 1:-1, :, :]
    )
    return along_x - 2.0 * padded[..., 1:-1, 1:-1, 1:-1]


def apply_batch(fields, conductivity, diagonal):
    stacked = jnp.concatenate((fields, conductivity[None] * fields), axis=0)
    padded = padded_2(stacked, (("px", 1), ("py", 2), ("pz", 3)), 1)
    half_count = fields.shape[0]
    near_sum = stencil_sum(padded[:half_count])
    far_sum = stencil_sum(padded[half_count:])
    return diagonal * fields - 0.5 * conductivity * near_sum - 0.5 * far_sum


def apply_vector(fields, conductivity, diagonal):
    stacked = jnp.concatenate((fields, conductivity[None] * fields), axis=0)
    padded = padded_2(stacked, (("px", 1), ("py", 2), ("pz", 3)), 1)
    near_sum = stencil_sum(padded[:1])
    far_sum = stencil_sum(padded[1:])
    return diagonal * fields - 0.5 * conductivity * near_sum - 0.5 * far_sum


def cholesky_low(gram):
    order = gram.shape[0]
    rows_idx = jnp.arange(order)
    factor = jnp.zeros((order, order), jnp.float32)
    for column in range(order):
        known = factor[:, :column]
        partial_sum = jnp.sum(known * known[column][None, :], axis=1)
        pivot = jnp.sqrt(gram[column, column] - partial_sum[column])
        values = (gram[:, column] - partial_sum) / pivot
        values = jnp.where(rows_idx > column, values, 0.0)
        factor = factor.at[:, column].set(values).at[column, column].set(pivot)
    return factor


def lower_inverse(factor):
    order = factor.shape[0]
    inverse = jnp.zeros((order, order), jnp.float32)
    for row in range(order):
        unit_row = jnp.zeros((order,), jnp.float32).at[row].set(1.0)
        partial_value = jnp.sum(factor[row, :row][:, None] * inverse[:row], axis=0)
        inverse = inverse.at[row].set((unit_row - partial_value) / factor[row, row])
    return inverse


def back_solve(upper_tri, target):
    order = upper_tri.shape[0]
    result = jnp.zeros((order,), jnp.float32)
    for row in range(order - 1, -1, -1):
        partial_value = jnp.sum(upper_tri[row, row + 1 :] * result[row + 1 :])
        result = result.at[row].set((target[row] - partial_value) / upper_tri[row, row])
    return result


def least_squares(hessenberg, beta_norm):
    upper_tri = hessenberg
    target = jnp.zeros((STEPS + 1,), jnp.float32).at[0].set(beta_norm)
    for column in range(STEPS):
        top_entry = upper_tri[column, column]
        low_entry = upper_tri[column + 1, column]
        radius = jnp.sqrt(top_entry * top_entry + low_entry * low_entry)
        cosine = top_entry / radius
        sine_val = low_entry / radius
        row_top = cosine * upper_tri[column] + sine_val * upper_tri[column + 1]
        row_low = cosine * upper_tri[column + 1] - sine_val * upper_tri[column]
        upper_tri = upper_tri.at[column].set(row_top).at[column + 1].set(row_low)
        goal_top = cosine * target[column] + sine_val * target[column + 1]
        goal_low = cosine * target[column + 1] - sine_val * target[column]
        target = target.at[column].set(goal_top).at[column + 1].set(goal_low)
    return back_solve(upper_tri[:STEPS], target[:STEPS])


def body(right_side, start_guess, conductivity, recycled):
    count_k = recycled.shape[0]
    block_shape = right_side.shape
    cell_count = right_side.size
    padded_cond = padded_2(conductivity, (("px", 0), ("py", 1), ("pz", 2)), 1)
    diagonal = shift_value + 7.0 * conductivity + 0.5 * stencil_sum(padded_cond)
    batch_in = jnp.concatenate((recycled, start_guess[None]), axis=0)
    images_all = apply_batch(batch_in, conductivity, diagonal)
    flat_images = images_all[:count_k].reshape(count_k, cell_count)
    first_residual = right_side.reshape(cell_count) - images_all[count_k].reshape(cell_count)
    gram = lax.psum(jnp.dot(flat_images, flat_images.T, precision=highest), ("px", "py", "pz"))
    factor_low = cholesky_low(gram)
    inverse = lower_inverse(factor_low)
    basis_c = jnp.dot(inverse, flat_images, precision=highest)
    projected = lax.psum(jnp.dot(basis_c, first_residual, precision=highest), ("px", "py", "pz"))
    recycle_flat = recycled.reshape(count_k, cell_count)
    solution = start_guess.reshape(cell_count) + jnp.dot(
        jnp.dot(inverse.T, projected, precision=highest), recycle_flat, precision=highest
    )
    residual = first_residual - jnp.dot(projected, basis_c, precision=highest)
    beta_norm = jnp.sqrt(
        lax.psum(jnp.dot(residual, residual, precision=highest), ("px", "py", "pz"))
    )
    basis_all = jnp.zeros((STEPS + 1, cell_count), jnp.float32).at[0].set(residual / beta_norm)
    coupling = jnp.zeros((count_k, STEPS), jnp.float32)
    hessenberg = jnp.zeros((STEPS + 1, STEPS), jnp.float32)
    for column in range(STEPS):
        current = basis_all[column].reshape((1,) + block_shape)
        vector_new = apply_vector(current, conductivity, diagonal).reshape(cell_count)
        known_basis = basis_all[: column + 1]
        coeff_c, coeff_v, whole_sq = lax.psum(
            (
                jnp.dot(basis_c, vector_new, precision=highest),
                jnp.dot(known_basis, vector_new, precision=highest),
                jnp.dot(vector_new, vector_new, precision=highest),
            ),
            ("px", "py", "pz"),
        )
        vector_new = (
            vector_new
            - jnp.dot(coeff_c, basis_c, precision=highest)
            - jnp.dot(coeff_v, known_basis, precision=highest)
        )
        norm_sq = (
            whole_sq
            - jnp.dot(coeff_c, coeff_c, precision=highest)
            - jnp.dot(coeff_v, coeff_v, precision=highest)
        )
        norm_new = jnp.sqrt(norm_sq)
        coupling = coupling.at[:, column].set(coeff_c)
        hessenberg = hessenberg.at[: column + 1, column].set(coeff_v)
        hessenberg = hessenberg.at[column + 1, column].set(norm_new)
        basis_all = basis_all.at[column + 1].set(vector_new / norm_new)
    coeffs = least_squares(hessenberg, beta_norm)
    recycle_coeffs = jnp.dot(
        inverse.T, jnp.dot(coupling, coeffs, precision=highest), precision=highest
    )
    solution = (
        solution
        + jnp.dot(coeffs, basis_all[:STEPS], precision=highest)
        - jnp.dot(recycle_coeffs, recycle_flat, precision=highest)
    )
    residual = residual - jnp.dot(
        jnp.dot(hessenberg, coeffs, precision=highest), basis_all, precision=highest
    )
    return (solution.reshape(block_shape), residual.reshape(block_shape), hessenberg)


def solution(mesh):
    return jax.shard_map(
        body,
        mesh=mesh,
        in_specs=(
            P("px", "py", "pz"),
            P("px", "py", "pz"),
            P("px", "py", "pz"),
            P(None, "px", "py", "pz"),
        ),
        out_specs=(P("px", "py", "pz"), P("px", "py", "pz"), P()),
        check_vma=False,
    )
```

profile of v0, /device:TPU:0, one launch (start us, length us, event | category | flops | bytes accessed | tf_op | source)
XLA Modules:
  0.0 911.4 jit_solution(14122070898462380592)
XLA Ops:
  3.0 5.0 collective-permute-start.6
  9.3 4.5 collective-permute-start
  37.9 4.6 collective-permute-start.8
  46.0 5.5 collective-permute-done.9
  72.8 6.4 maximum_maximum_fusion
  82.7 42.2 %psum.189 = f32[16,16]{1,0:T(8,128)S(1)} all-reduce(f32[16,16]{1,0:T(8,128)S(1)} %convolution_bitcast_fusion), channel_id=1, replica_groups=mesh['px'=4,'py'=4,'pz'=2] {'px','py','pz'}, use_global_device_ids=true, to_apply=%region_1.2 | all-reduce | flops 256 | bytes 2048 | tf_op jit(solution)/shard_map/psum | solution.py:117
  187.5 39.8 %psum.190 = f32[16]{0:T(128)S(1)} all-reduce(f32[16]{0:T(128)S(1)} %convolution_bitcast_fusion.20), channel_id=1, replica_groups=mesh['px'=4,'py'=4,'pz'=2] {'px','py','pz'}, use_global_device_ids=true, to_apply=%region_44.45 | all-reduce | flops 16 | bytes 128 | tf_op jit(solution)/shard_map/psum | solution.py:121
  228.2 40.2 %psum.191 = f32[]{:T(128)} all-reduce(f32[]{:T(128)} %get-tuple-element.1699), channel_id=1, replica_groups=mesh['px'=4,'py'=4,'pz'=2] {'px','py','pz'}, use_global_device_ids=true, to_apply=%region_45.46 | all-reduce | flops 1 | bytes 8 | tf_op jit(solution)/shard_map/psum | solution.py:128
  274.7 3.7 collective-permute-done.13
  278.5 4.2 collective-permute-start.14
  284.0 4.2 collective-permute-done.15
  295.2 40.4 %all-reduce.14 = (f32[16]{0:T(128)S(1)}, f32[]{:T(128)}, f32[1]{0:T(128)}) all-reduce(f32[16]{0:T(128)S(1)} %convolution_bitcast_fusion.19, f32[]{:T(128)} %get-tuple-element.1697, f32[1]{0:T(128)} %bitcast.135), channel_id=1, replica_groups=mesh['px'=4,'py'=4,'pz'=2] {'px','py','pz'}, use_global_device_ids=true, to_apply=%region_48.49 | all-reduce | flops 18 | bytes 144 | tf_op jit(solution)/shard_map/psum | solution.py:137
  344.4 4.2 collective-permute-done.19
  348.7 4.2 collective-permute-start.20
  365.5 39.3 %all-reduce.13 = (f32[16]{0:T(128)S(1)}, f32[2]{0:T(128)S(1)}, f32[]{:T(128)}) all-reduce(f32[16]{0:T(128)S(1)} %convolution_bitcast_fusion.17, f32[2]{0:T(128)S(1)} %convolution_bitcast_fusion.18, f32[]{:T(128)} %get-tuple-element.1695), channel_id=1, replica_groups=mesh['px'=4,'py'=4,'pz'=2] {'px','py','pz'}, use_global_device_ids=true, to_apply=%region_52.53 | all-reduce | flops 19 | bytes 152 | tf_op jit(solution)/shard_map/psum | solution.py:137
  414.5 3.7 collective-permute-done.25
  418.3 4.2 collective-permute-start.26
  423.8 4.2 collective-permute-done.27
  435.1 39.3 %all-reduce.12 = (f32[16]{0:T(128)S(1)}, f32[3]{0:T(128)S(1)}, f32[]{:T(128)}) all-reduce(f32[16]{0:T(128)S(1)} %convolution_bitcast_fusion.15, f32[3]{0:T(128)S(1)} %convolution_bitcast_fusion.16, f32[]{:T(128)} %get-tuple-element.1693), channel_id=1, replica_groups=mesh['px'=4,'py'=4,'pz'=2] {'px','py','pz'}, use_global_device_ids=true, to_apply=%region_56.57 | all-reduce | flops 20 | bytes 160 | tf_op jit(solution)/shard_map/psum | solution.py:137
  483.0 4.2 collective-permute-done.31
  487.3 4.2 collective-permute-start.32
  504.3 41.2 %all-reduce.11 = (f32[16]{0:T(128)S(1)}, f32[4]{0:T(128)S(1)}, f32[]{:T(128)}) all-reduce(f32[16]{0:T(128)S(1)} %convolution_bitcast_fusion.13, f32[4]{0:T(128)S(1)} %convolution_bitcast_fusion.14, f32[]{:T(128)} %get-tuple-element.1691), channel_id=1, replica_groups=mesh['px'=4,'py'=4,'pz'=2] {'px','py','pz'}, use_global_device_ids=true, to_apply=%region_60.61 | all-reduce | flops 21 | bytes 168 | tf_op jit(solution)/shard_map/psum | solution.py:137
  558.3 4.2 collective-permute-start.38
  575.1 40.1 %all-reduce.10 = (f32[16]{0:T(128)S(1)}, f32[5]{0:T(128)S(1)}, f32[]{:T(128)}) all-reduce(f32[16]{0:T(128)S(1)} %convolution_bitcast_fusion.11, f32[5]{0:T(128)S(1)} %convolution_bitcast_fusion.12, f32[]{:T(128)} %get-tuple-element.1689), channel_id=1, replica_groups=mesh['px'=4,'py'=4,'pz'=2] {'px','py','pz'}, use_global_device_ids=true, to_apply=%region_64.65 | all-reduce | flops 22 | bytes 176 | tf_op jit(solution)/shard_map/psum | solution.py:137
  627.9 4.2 collective-permute-start.44
  646.5 41.4 %all-reduce.9 = (f32[16]{0:T(128)S(1)}, f32[6]{0:T(128)S(1)}, f32[]{:T(128)}) all-reduce(f32[16]{0:T(128)S(1)} %convolution_bitcast_fusion.9, f32[6]{0:T(128)S(1)} %convolution_bitcast_fusion.10, f32[]{:T(128)} %get-tuple-element.1687), channel_id=1, replica_groups=mesh['px'=4,'py'=4,'pz'=2] {'px','py','pz'}, use_global_device_ids=true, to_apply=%region_68.69 | all-reduce | flops 23 | bytes 184 | tf_op jit(solution)/shard_map/psum | solution.py:137
  696.4 3.7 collective-permute-done.49
  700.1 4.2 collective-permute-start.50
  717.0 40.6 %all-reduce.8 = (f32[16]{0:T(128)S(1)}, f32[7]{0:T(128)S(1)}, f32[]{:T(128)}) all-reduce(f32[16]{0:T(128)S(1)} %convolution_bitcast_fusion.7, f32[7]{0:T(128)S(1)} %convolution_bitcast_fusion.8, f32[]{:T(128)} %get-tuple-element.1685), channel_id=1, replica_groups=mesh['px'=4,'py'=4,'pz'=2] {'px','py','pz'}, use_global_device_ids=true, to_apply=%region_72.73 | all-reduce | flops 24 | bytes 192 | tf_op jit(solution)/shard_map/psum | solution.py:137
  769.7 4.2 collective-permute-start.56
  775.8 3.6 collective-permute-done.57
  788.4 41.4 %all-reduce.7 = (f32[16]{0:T(128)S(1)}, f32[8]{0:T(128)S(1)}, f32[]{:T(128)}) all-reduce(f32[16]{0:T(128)S(1)} %convolution_bitcast_fusion.5, f32[8]{0:T(128)S(1)} %convolution_bitcast_fusion.6, f32[]{:T(128)} %get-tuple-element.1683), channel_id=1, replica_groups=mesh['px'=4,'py'=4,'pz'=2] {'px','py','pz'}, use_global_device_ids=true, to_apply=%region_76.77 | all-reduce | flops 25 | bytes 200 | tf_op jit(solution)/shard_map/psum | solution.py:137
  (665 shorter events, 283.4 us)
Async XLA Ops:
  3.0 34.8 %collective-permute-start.6 = (f32[34,1,16,128]{3,0,2,1:T(8,128)S(1)}, f32[34,1,16,128]{3,0,2,1:T(8,128)S(1)}, u32[]{:S(2)}, u32[]{:S(2)}) collective-permute-start(f32[34,1,16,128]{3,0,2,1:T(8,128)S(1)} %get-tuple-element.1711), channel_id=1, source_target_pairs={{0,8},{8,16},{16,24},{1,9},{9,17},{17,25},{2,10},{10,18},{18,26},{... | collective-permute-start | bytes 835592 | tf_op jit(solution)/shard_map/ppermute | solution.py:20
  8.0 29.9 %collective-permute-start.7 = (f32[34,1,16,128]{3,0,2,1:T(8,128)S(1)}, f32[34,1,16,128]{3,0,2,1:T(8,128)S(1)}, u32[]{:S(2)}, u32[]{:S(2)}) collective-permute-start(f32[34,1,16,128]{3,0,2,1:T(8,128)S(1)} %get-tuple-element.1712), channel_id=1, source_target_pairs={{8,0},{16,8},{24,16},{9,1},{17,9},{25,17},{10,2},{18,10},{26,18},{... | collective-permute-start | bytes 835592 | tf_op jit(solution)/shard_map/ppermute | solution.py:21
  9.3 10.0 %collective-permute-start = (f32[1,16,128]{2,1,0:T(8,128)S(1)}, f32[1,16,128]{2,1,0:T(8,128)S(1)}, u32[]{:S(2)}, u32[]{:S(2)}) collective-permute-start(f32[1,16,128]{2,1,0:T(8,128)S(1)} %get-tuple-element.1768), channel_id=1, source_target_pairs={{0,8},{8,16},{16,24},{1,9},{9,17},{17,25},{2,10},{10,18},{18,26},{... | collective-permute-start | bytes 24584 | tf_op jit(solution)/shard_map/ppermute | solution.py:20
  13.9 5.5 collective-permute-start.1
  19.5 12.8 %collective-permute-start.2 = (f32[6,1,128]{2,1,0:T(1,128)S(1)}, f32[6,1,128]{2,1,0:T(1,128)S(1)}, u32[]{:S(2)}, u32[]{:S(2)}) collective-permute-start(f32[6,1,128]{2,1,0:T(1,128)S(1)} %get-tuple-element.1763), channel_id=1, source_target_pairs={{0,2},{2,4},{4,6},{1,3},{3,5},{5,7},{8,10},{10,12},{12,14},{9,11},... | collective-permute-start | bytes 9224 | tf_op jit(solution)/shard_map/ppermute | solution.py:20
  22.9 9.4 %collective-permute-start.3 = (f32[6,1,128]{2,1,0:T(1,128)S(1)}, f32[6,1,128]{2,1,0:T(1,128)S(1)}, u32[]{:S(2)}, u32[]{:S(2)}) collective-permute-start(f32[6,1,128]{2,1,0:T(1,128)S(1)} %get-tuple-element.1764), channel_id=1, source_target_pairs={{2,0},{4,2},{6,4},{3,1},{5,3},{7,5},{10,8},{12,10},{14,12},{11,9},... | collective-permute-start | bytes 9224 | tf_op jit(solution)/shard_map/ppermute | solution.py:21
  37.9 8.1 collective-permute-start.8
  42.5 9.0 collective-permute-start.9
  58.2 8.5 collective-permute-start.10
  63.9 5.9 collective-permute-start.11
  272.8 5.6 collective-permute-start.13
  282.6 5.5 collective-permute-start.15
  343.0 5.6 collective-permute-start.19
  348.7 6.2 collective-permute-start.20
  352.9 5.5 collective-permute-start.21
  412.6 5.6 collective-permute-start.25
  422.5 5.5 collective-permute-start.27
  481.6 5.6 collective-permute-start.31
  487.3 9.5 %collective-permute-start.32 = (f32[2,6,1,128]{3,2,1,0:T(1,128)S(1)}, f32[2,6,1,128]{3,2,1,0:T(1,128)S(1)}, u32[]{:S(2)}, u32[]{:S(2)}) collective-permute-start(f32[2,6,1,128]{3,2,1,0:T(1,128)S(1)} %get-tuple-element.1737), channel_id=1, source_target_pairs={{0,2},{2,4},{4,6},{1,3},{3,5},{5,7},{8,10},{10,12},{12,14},{9,11},... | collective-permute-start | bytes 18440 | tf_op jit(solution)/shard_map/ppermute | solution.py:20
  549.4 6.0 collective-permute-start.36
  552.6 5.6 collective-permute-start.37
  558.3 9.1 %collective-permute-start.38 = (f32[2,6,1,128]{3,2,1,0:T(1,128)S(1)}, f32[2,6,1,128]{3,2,1,0:T(1,128)S(1)}, u32[]{:S(2)}, u32[]{:S(2)}) collective-permute-start(f32[2,6,1,128]{3,2,1,0:T(1,128)S(1)} %get-tuple-element.1735), channel_id=1, source_target_pairs={{0,2},{2,4},{4,6},{1,3},{3,5},{5,7},{8,10},{10,12},{12,14},{9,11},... | collective-permute-start | bytes 18440 | tf_op jit(solution)/shard_map/ppermute | solution.py:20
  619.1 8.1 collective-permute-start.42
  622.3 5.6 collective-permute-start.43
  627.9 6.1 collective-permute-start.44
  637.8 6.3 collective-permute-start.46
  694.5 5.6 collective-permute-start.49
  700.1 9.1 %collective-permute-start.50 = (f32[2,6,1,128]{3,2,1,0:T(1,128)S(1)}, f32[2,6,1,128]{3,2,1,0:T(1,128)S(1)}, u32[]{:S(2)}, u32[]{:S(2)}) collective-permute-start(f32[2,6,1,128]{3,2,1,0:T(1,128)S(1)} %get-tuple-element.1731), channel_id=1, source_target_pairs={{0,2},{2,4},{4,6},{1,3},{3,5},{5,7},{8,10},{10,12},{12,14},{9,11},... | collective-permute-start | bytes 18440 | tf_op jit(solution)/shard_map/ppermute | solution.py:20
  761.5 7.4 collective-permute-start.54
  764.0 5.6 collective-permute-start.55
  769.7 6.1 collective-permute-start.56
  779.5 6.4 collective-permute-start.58
  (62 other events, 2085.2 us)
where the time goes:
time: 925 us; the launch traced here: 911 us
  blocking collectives  446 us (48%)
  starting transfers between devices  128 us (14%)
  other arithmetic  98.5 us (11%)
  between operations  91.1 us (10%)
  local copies, waits for them, and re-layouts  68.2 us (7%)
  waiting for transfers between devices  58.2 us (6%)
  matrix products  21.4 us (2%)
    psum x8, blocking collectives, body(): lax.psum((jnp.dot(basis_c, vector_new, precision=highest), jnp.dot(known_...  324 us
    ppermute x30, starting transfers between devices, padded_2(): before = lax.ppermute(last, axis, up)  89.3 us
    ppermute x30, waiting for transfers between devices, padded_2(): after = lax.ppermute(leading, axis, down)  56.3 us
    another operation x61, other arithmetic  46.9 us
    psum x1, blocking collectives, body(): lax.psum(jnp.dot(flat_images, flat_images.T, precision=highest), ('px', '...  42.2 us
    psum x1, blocking collectives, body(): lax.psum(jnp.dot(residual, residual, precision=highest), ('px', 'py', 'pz'))  40.2 us
    psum x1, blocking collectives, body(): lax.psum(jnp.dot(basis_c, first_residual, precision=highest), ('px', 'py'...  39.8 us
    ppermute x30, starting transfers between devices, padded_2(): after = lax.ppermute(leading, axis, down)  38.8 us
  transfers between devices with their start and end apart: 60, of which 27 were waited for; matrix products, arithmetic and copies ran while one was open for 7% of the time, Pallas kernels for 0%

commit v1 on v0

--- a/solution.py
+++ b/solution.py
@@ -1,3 +1,4 @@
+import functools
 import jax
 import jax.numpy as jnp
 from jax import lax
@@ -8,6 +9,14 @@
 edge_weight = 0.25 ** (1.0 / 3.0)
 middle_weight = 2.0 * edge_weight
 shift_value = 0.4
+
+
+def pass_group_over_axis(view, link_axis, shard_axis):
+    block_last = lax.psum(lax.psum(view, axis_name=link_axis), axis_name=shard_axis)
+    return block_last
+
+
+links_cover = functools.partial(pass_group_over_axis, link_axis=("py", "pz"), shard_axis="px")
 
 
 def padded_2(array, sides, width):
@@ -134,13 +143,12 @@
         current = basis_all[column].reshape((1,) + block_shape)
         vector_new = apply_vector(current, conductivity, diagonal).reshape(cell_count)
         known_basis = basis_all[: column + 1]
-        coeff_c, coeff_v, whole_sq = lax.psum(
+        coeff_c, coeff_v, whole_sq = links_cover(
             (
                 jnp.dot(basis_c, vector_new, precision=highest),
                 jnp.dot(known_basis, vector_new, precision=highest),
                 jnp.dot(vector_new, vector_new, precision=highest),
-            ),
-            ("px", "py", "pz"),
+            )
         )
         vector_new = (
             vector_new

time: 925 us -> 793 us (0.86)
  blocking collectives: 446 us -> 309 us
  waiting for transfers between devices: 58.2 us -> 71.4 us
    psum x8 -> x16, blocking collectives: 324 us -> 187 us  [the longest x8 108 us: pass_group_over_axis(): lax.psum(view, axis_name=link_axis)]
    ppermute x30, waiting for transfers between devices: 56.3 us -> 69.5 us  [padded_2(): after = lax.ppermute(leading, axis, down)]
  transfers between devices with their start and end apart: 60 -> 60, of which waited for: 27 -> 27; matrix products, arithmetic and copies ran while one was open for 7% -> 8% of each run, Pallas kernels for 0% -> 0%
where the time goes in v1:
time: 793 us; the launch traced here: 779 us
  blocking collectives  309 us (39%)
  starting transfers between devices  120 us (15%)
  other arithmetic  98.3 us (12%)
  between operations  91.2 us (12%)
  waiting for transfers between devices  71.4 us (9%)
  local copies, waits for them, and re-layouts  67.8 us (9%)
  matrix products  21.4 us (3%)
    psum x8, blocking collectives, pass_group_over_axis(): lax.psum(view, axis_name=link_axis)  108 us
    ppermute x30, starting transfers between devices, padded_2(): before = lax.ppermute(last, axis, up)  80.9 us
    psum x8, blocking collectives, pass_group_over_axis(): lax.psum(lax.psum(view, axis_name=link_axis), axis_name=shard_axis)  78.1 us
    ppermute x30, waiting for transfers between devices, padded_2(): after = lax.ppermute(leading, axis, down)  69.5 us
    another operation x61, other arithmetic  46.8 us
    psum x1, blocking collectives, body(): lax.psum(jnp.dot(flat_images, flat_images.T, precision=highest), ('px', '...  42.2 us
    psum x1, blocking collectives, body(): lax.psum(jnp.dot(residual, residual, precision=highest), ('px', 'py', 'pz'))  40.3 us
    psum x1, blocking collectives, body(): lax.psum(jnp.dot(basis_c, first_residual, precision=highest), ('px', 'py'...  39.8 us
  transfers between devices with their start and end apart: 60, of which 27 were waited for; matrix products, arithmetic and copies ran while one was open for 8% of the time, Pallas kernels for 0%

profile of v1, /device:TPU:0, one launch (start us, length us, event | category | flops | bytes accessed | tf_op | source)
XLA Modules:
  0.0 779.1 jit_solution(3895736077826692933)
XLA Ops:
  3.0 5.0 collective-permute-start.6
  9.3 4.5 collective-permute-start
  37.9 4.6 collective-permute-start.8
  46.0 5.5 collective-permute-done.9
  72.8 6.4 maximum_maximum_fusion
  82.7 42.2 %psum.357 = f32[16,16]{1,0:T(8,128)S(1)} all-reduce(f32[16,16]{1,0:T(8,128)S(1)} %convolution_bitcast_fusion), channel_id=1, replica_groups=mesh['px'=4,'py'=4,'pz'=2] {'px','py','pz'}, use_global_device_ids=true, to_apply=%region_1.2 | all-reduce | flops 256 | bytes 2048 | tf_op jit(solution)/shard_map/psum | solution.py:126
  187.5 39.8 %psum.358 = f32[16]{0:T(128)S(1)} all-reduce(f32[16]{0:T(128)S(1)} %convolution_bitcast_fusion.20), channel_id=1, replica_groups=mesh['px'=4,'py'=4,'pz'=2] {'px','py','pz'}, use_global_device_ids=true, to_apply=%region_44.45 | all-reduce | flops 16 | bytes 128 | tf_op jit(solution)/shard_map/psum | solution.py:130
  228.3 40.3 %psum.359 = f32[]{:T(128)} all-reduce(f32[]{:T(128)} %get-tuple-element.1723), channel_id=1, replica_groups=mesh['px'=4,'py'=4,'pz'=2] {'px','py','pz'}, use_global_device_ids=true, to_apply=%region_45.46 | all-reduce | flops 1 | bytes 8 | tf_op jit(solution)/shard_map/psum | solution.py:137
  278.5 4.2 collective-permute-start.14
  284.0 4.2 collective-permute-done.15
  295.2 12.9 %all-reduce.14 = (f32[16]{0:T(128)S(1)}, f32[]{:T(128)}, f32[1]{0:T(128)}) all-reduce(f32[16]{0:T(128)S(1)} %convolution_bitcast_fusion.19, f32[]{:T(128)} %get-tuple-element.1721, f32[1]{0:T(128)} %bitcast.135), channel_id=1, replica_groups=mesh['px'=4,'py'=4,'pz'=2] {'py','pz'}, use_global_device_ids=true, to_apply=%region_50.51 | all-reduce | flops 18 | bytes 144 | tf_op jit(solution)/shard_map/psum | solution.py:15
  308.2 10.4 %all-reduce.22 = (f32[16]{0:T(128)S(1)}, f32[]{:T(128)}, f32[1]{0:T(128)}) all-reduce(f32[16]{0:T(128)S(1)} %get-tuple-element.1680, f32[]{:T(128)} %get-tuple-element.1681, f32[1]{0:T(128)} %get-tuple-element.1682), channel_id=1, replica_groups=mesh['px'=4,'py'=4,'pz'=2] {'px'}, use_global_device_ids=true, to_apply=%region_51.52 | all-reduce | flops 18 | bytes 144 | tf_op jit(solution)/shard_map/psum | solution.py:15
  327.3 4.2 collective-permute-done.19
  336.7 5.4 collective-permute-done.21
  349.2 12.7 %all-reduce.13 = (f32[16]{0:T(128)S(1)}, f32[2]{0:T(128)S(1)}, f32[]{:T(128)}) all-reduce(f32[16]{0:T(128)S(1)} %convolution_bitcast_fusion.17, f32[2]{0:T(128)S(1)} %convolution_bitcast_fusion.18, f32[]{:T(128)} %get-tuple-element.1719), channel_id=1, replica_groups=mesh['px'=4,'py'=4,'pz'=2] {'py','pz'}, use_global_device_ids=true, to_apply=%region_57.58 | all-reduce | flops 19 | bytes 152 | tf_op jit(solution)/shard_map/psum | solution.py:15
  361.9 9.0 %all-reduce.21 = (f32[16]{0:T(128)S(1)}, f32[2]{0:T(128)S(1)}, f32[]{:T(128)}) all-reduce(f32[16]{0:T(128)S(1)} %get-tuple-element.1677, f32[2]{0:T(128)S(1)} %get-tuple-element.1678, f32[]{:T(128)} %get-tuple-element.1679), channel_id=1, replica_groups=mesh['px'=4,'py'=4,'pz'=2] {'px'}, use_global_device_ids=true, to_apply=%region_58.59 | all-reduce | flops 19 | bytes 152 | tf_op jit(solution)/shard_map/psum | solution.py:15
  389.7 6.1 collective-permute-done.27
  403.0 12.6 %all-reduce.12 = (f32[16]{0:T(128)S(1)}, f32[3]{0:T(128)S(1)}, f32[]{:T(128)}) all-reduce(f32[16]{0:T(128)S(1)} %convolution_bitcast_fusion.15, f32[3]{0:T(128)S(1)} %convolution_bitcast_fusion.16, f32[]{:T(128)} %get-tuple-element.1717), channel_id=1, replica_groups=mesh['px'=4,'py'=4,'pz'=2] {'py','pz'}, use_global_device_ids=true, to_apply=%region_64.65 | all-reduce | flops 20 | bytes 160 | tf_op jit(solution)/shard_map/psum | solution.py:15
  415.6 9.0 %all-reduce.20 = (f32[16]{0:T(128)S(1)}, f32[3]{0:T(128)S(1)}, f32[]{:T(128)}) all-reduce(f32[16]{0:T(128)S(1)} %get-tuple-element.1674, f32[3]{0:T(128)S(1)} %get-tuple-element.1675, f32[]{:T(128)} %get-tuple-element.1676), channel_id=1, replica_groups=mesh['px'=4,'py'=4,'pz'=2] {'px'}, use_global_device_ids=true, to_apply=%region_65.66 | all-reduce | flops 20 | bytes 160 | tf_op jit(solution)/shard_map/psum | solution.py:15
  433.9 4.2 collective-permute-done.31
  456.3 14.7 %all-reduce.11 = (f32[16]{0:T(128)S(1)}, f32[4]{0:T(128)S(1)}, f32[]{:T(128)}) all-reduce(f32[16]{0:T(128)S(1)} %convolution_bitcast_fusion.13, f32[4]{0:T(128)S(1)} %convolution_bitcast_fusion.14, f32[]{:T(128)} %get-tuple-element.1715), channel_id=1, replica_groups=mesh['px'=4,'py'=4,'pz'=2] {'py','pz'}, use_global_device_ids=true, to_apply=%region_71.72 | all-reduce | flops 21 | bytes 168 | tf_op jit(solution)/shard_map/psum | solution.py:15
  471.0 9.0 %all-reduce.19 = (f32[16]{0:T(128)S(1)}, f32[4]{0:T(128)S(1)}, f32[]{:T(128)}) all-reduce(f32[16]{0:T(128)S(1)} %get-tuple-element.1671, f32[4]{0:T(128)S(1)} %get-tuple-element.1672, f32[]{:T(128)} %get-tuple-element.1673), channel_id=1, replica_groups=mesh['px'=4,'py'=4,'pz'=2] {'px'}, use_global_device_ids=true, to_apply=%region_72.73 | all-reduce | flops 21 | bytes 168 | tf_op jit(solution)/shard_map/psum | solution.py:15
  509.3 14.2 %all-reduce.10 = (f32[16]{0:T(128)S(1)}, f32[5]{0:T(128)S(1)}, f32[]{:T(128)}) all-reduce(f32[16]{0:T(128)S(1)} %convolution_bitcast_fusion.11, f32[5]{0:T(128)S(1)} %convolution_bitcast_fusion.12, f32[]{:T(128)} %get-tuple-element.1713), channel_id=1, replica_groups=mesh['px'=4,'py'=4,'pz'=2] {'py','pz'}, use_global_device_ids=true, to_apply=%region_78.79 | all-reduce | flops 22 | bytes 176 | tf_op jit(solution)/shard_map/psum | solution.py:15
  523.5 9.0 %all-reduce.18 = (f32[16]{0:T(128)S(1)}, f32[5]{0:T(128)S(1)}, f32[]{:T(128)}) all-reduce(f32[16]{0:T(128)S(1)} %get-tuple-element.1668, f32[5]{0:T(128)S(1)} %get-tuple-element.1669, f32[]{:T(128)} %get-tuple-element.1670), channel_id=1, replica_groups=mesh['px'=4,'py'=4,'pz'=2] {'px'}, use_global_device_ids=true, to_apply=%region_79.80 | all-reduce | flops 22 | bytes 176 | tf_op jit(solution)/shard_map/psum | solution.py:15
  549.8 5.4 collective-permute-done.45
  564.0 13.6 %all-reduce.9 = (f32[16]{0:T(128)S(1)}, f32[6]{0:T(128)S(1)}, f32[]{:T(128)}) all-reduce(f32[16]{0:T(128)S(1)} %convolution_bitcast_fusion.9, f32[6]{0:T(128)S(1)} %convolution_bitcast_fusion.10, f32[]{:T(128)} %get-tuple-element.1711), channel_id=1, replica_groups=mesh['px'=4,'py'=4,'pz'=2] {'py','pz'}, use_global_device_ids=true, to_apply=%region_85.86 | all-reduce | flops 23 | bytes 184 | tf_op jit(solution)/shard_map/psum | solution.py:15
  577.6 11.3 %all-reduce.17 = (f32[16]{0:T(128)S(1)}, f32[6]{0:T(128)S(1)}, f32[]{:T(128)}) all-reduce(f32[16]{0:T(128)S(1)} %get-tuple-element.1665, f32[6]{0:T(128)S(1)} %get-tuple-element.1666, f32[]{:T(128)} %get-tuple-element.1667), channel_id=1, replica_groups=mesh['px'=4,'py'=4,'pz'=2] {'px'}, use_global_device_ids=true, to_apply=%region_86.87 | all-reduce | flops 23 | bytes 184 | tf_op jit(solution)/shard_map/psum | solution.py:15
  618.1 14.2 %all-reduce.8 = (f32[16]{0:T(128)S(1)}, f32[7]{0:T(128)S(1)}, f32[]{:T(128)}) all-reduce(f32[16]{0:T(128)S(1)} %convolution_bitcast_fusion.7, f32[7]{0:T(128)S(1)} %convolution_bitcast_fusion.8, f32[]{:T(128)} %get-tuple-element.1709), channel_id=1, replica_groups=mesh['px'=4,'py'=4,'pz'=2] {'py','pz'}, use_global_device_ids=true, to_apply=%region_92.93 | all-reduce | flops 24 | bytes 192 | tf_op jit(solution)/shard_map/psum | solution.py:15
  632.3 9.5 %all-reduce.16 = (f32[16]{0:T(128)S(1)}, f32[7]{0:T(128)S(1)}, f32[]{:T(128)}) all-reduce(f32[16]{0:T(128)S(1)} %get-tuple-element.1662, f32[7]{0:T(128)S(1)} %get-tuple-element.1663, f32[]{:T(128)} %get-tuple-element.1664), channel_id=1, replica_groups=mesh['px'=4,'py'=4,'pz'=2] {'px'}, use_global_device_ids=true, to_apply=%region_93.94 | all-reduce | flops 24 | bytes 192 | tf_op jit(solution)/shard_map/psum | solution.py:15
  658.6 5.4 collective-permute-done.57
  672.9 13.6 %all-reduce.7 = (f32[16]{0:T(128)S(1)}, f32[8]{0:T(128)S(1)}, f32[]{:T(128)}) all-reduce(f32[16]{0:T(128)S(1)} %convolution_bitcast_fusion.5, f32[8]{0:T(128)S(1)} %convolution_bitcast_fusion.6, f32[]{:T(128)} %get-tuple-element.1707), channel_id=1, replica_groups=mesh['px'=4,'py'=4,'pz'=2] {'py','pz'}, use_global_device_ids=true, to_apply=%region_99.100 | all-reduce | flops 25 | bytes 200 | tf_op jit(solution)/shard_map/psum | solution.py:15
  686.4 10.9 %all-reduce.15 = (f32[16]{0:T(128)S(1)}, f32[8]{0:T(128)S(1)}, f32[]{:T(128)}) all-reduce(f32[16]{0:T(128)S(1)} %get-tuple-element.1659, f32[8]{0:T(128)S(1)} %get-tuple-element.1660, f32[]{:T(128)} %get-tuple-element.1661), channel_id=1, replica_groups=mesh['px'=4,'py'=4,'pz'=2] {'px'}, use_global_device_ids=true, to_apply=%region_100.101 | all-reduce | flops 25 | bytes 200 | tf_op jit(solution)/shard_map/psum | solution.py:15
  (673 shorter events, 313.9 us)
Async XLA Ops:
  3.0 34.8 %collective-permute-start.6 = (f32[34,1,16,128]{3,0,2,1:T(8,128)S(1)}, f32[34,1,16,128]{3,0,2,1:T(8,128)S(1)}, u32[]{:S(2)}, u32[]{:S(2)}) collective-permute-start(f32[34,1,16,128]{3,0,2,1:T(8,128)S(1)} %get-tuple-element.1735), channel_id=1, source_target_pairs={{0,8},{8,16},{16,24},{1,9},{9,17},{17,25},{2,10},{10,18},{18,26},{... | collective-permute-start | bytes 835592 | tf_op jit(solution)/shard_map/ppermute | solution.py:29
  8.0 29.9 %collective-permute-start.7 = (f32[34,1,16,128]{3,0,2,1:T(8,128)S(1)}, f32[34,1,16,128]{3,0,2,1:T(8,128)S(1)}, u32[]{:S(2)}, u32[]{:S(2)}) collective-permute-start(f32[34,1,16,128]{3,0,2,1:T(8,128)S(1)} %get-tuple-element.1736), channel_id=1, source_target_pairs={{8,0},{16,8},{24,16},{9,1},{17,9},{25,17},{10,2},{18,10},{26,18},{... | collective-permute-start | bytes 835592 | tf_op jit(solution)/shard_map/ppermute | solution.py:30
  9.3 10.0 %collective-permute-start = (f32[1,16,128]{2,1,0:T(8,128)S(1)}, f32[1,16,128]{2,1,0:T(8,128)S(1)}, u32[]{:S(2)}, u32[]{:S(2)}) collective-permute-start(f32[1,16,128]{2,1,0:T(8,128)S(1)} %get-tuple-element.1792), channel_id=1, source_target_pairs={{0,8},{8,16},{16,24},{1,9},{9,17},{17,25},{2,10},{10,18},{18,26},{... | collective-permute-start | bytes 24584 | tf_op jit(solution)/shard_map/ppermute | solution.py:29
  19.5 12.8 %collective-permute-start.2 = (f32[6,1,128]{2,1,0:T(1,128)S(1)}, f32[6,1,128]{2,1,0:T(1,128)S(1)}, u32[]{:S(2)}, u32[]{:S(2)}) collective-permute-start(f32[6,1,128]{2,1,0:T(1,128)S(1)} %get-tuple-element.1787), channel_id=1, source_target_pairs={{0,2},{2,4},{4,6},{1,3},{3,5},{5,7},{8,10},{10,12},{12,14},{9,11},... | collective-permute-start | bytes 9224 | tf_op jit(solution)/shard_map/ppermute | solution.py:29
  22.9 9.4 %collective-permute-start.3 = (f32[6,1,128]{2,1,0:T(1,128)S(1)}, f32[6,1,128]{2,1,0:T(1,128)S(1)}, u32[]{:S(2)}, u32[]{:S(2)}) collective-permute-start(f32[6,1,128]{2,1,0:T(1,128)S(1)} %get-tuple-element.1788), channel_id=1, source_target_pairs={{2,0},{4,2},{6,4},{3,1},{5,3},{7,5},{10,8},{12,10},{14,12},{11,9},... | collective-permute-start | bytes 9224 | tf_op jit(solution)/shard_map/ppermute | solution.py:30
  37.9 8.1 %collective-permute-start.8 = (f32[34,6,1,128]{3,0,2,1:T(8,128)S(1)}, f32[34,6,1,128]{3,0,2,1:T(8,128)S(1)}, u32[]{:S(2)}, u32[]{:S(2)}) collective-permute-start(f32[34,6,1,128]{3,0,2,1:T(8,128)S(1)} %get-tuple-element.1733), channel_id=1, source_target_pairs={{0,2},{2,4},{4,6},{1,3},{3,5},{5,7},{8,10},{10,12},{12,14},{9,11},... | collective-permute-start | bytes 313352 | tf_op jit(solution)/shard_map/ppermute | solution.py:29
  42.5 9.0 %collective-permute-start.9 = (f32[34,6,1,128]{3,0,2,1:T(8,128)S(1)}, f32[34,6,1,128]{3,0,2,1:T(8,128)S(1)}, u32[]{:S(2)}, u32[]{:S(2)}) collective-permute-start(f32[34,6,1,128]{3,0,2,1:T(8,128)S(1)} %get-tuple-element.1734), channel_id=1, source_target_pairs={{2,0},{4,2},{6,4},{3,1},{5,3},{7,5},{10,8},{12,10},{14,12},{11,9},... | collective-permute-start | bytes 313352 | tf_op jit(solution)/shard_map/ppermute | solution.py:30
  58.2 8.5 %collective-permute-start.10 = (f32[34,6,18,1]{0,3,2,1:T(1,128)}, f32[34,6,18,1]{0,3,2,1:T(1,128)}, u32[]{:S(2)}, u32[]{:S(2)}) collective-permute-start(f32[34,6,18,1]{0,3,2,1:T(1,128)} %copy.40), channel_id=1, source_target_pairs={{0,1},{2,3},{4,5},{6,7},{8,9},{10,11},{12,13},{14,15},{16,17},{18,... | collective-permute-start | bytes 44072 | tf_op jit(solution)/shard_map/ppermute | solution.py:29
  63.9 5.9 collective-permute-start.11
  272.8 5.6 collective-permute-start.13
  325.9 5.6 collective-permute-start.19
  334.7 7.4 collective-permute-start.21
  375.5 5.8 collective-permute-start.24
  379.3 5.6 collective-permute-start.25
  388.4 7.5 collective-permute-start.27
  432.5 5.6 collective-permute-start.31
  438.2 8.8 %collective-permute-start.32 = (f32[2,6,1,128]{3,2,1,0:T(1,128)S(1)}, f32[2,6,1,128]{3,2,1,0:T(1,128)S(1)}, u32[]{:S(2)}, u32[]{:S(2)}) collective-permute-start(f32[2,6,1,128]{3,2,1,0:T(1,128)S(1)} %get-tuple-element.1761), channel_id=1, source_target_pairs={{0,2},{2,4},{4,6},{1,3},{3,5},{5,7},{8,10},{10,12},{12,14},{9,11},... | collective-permute-start | bytes 18440 | tf_op jit(solution)/shard_map/ppermute | solution.py:29
  441.7 7.4 collective-permute-start.33
  483.8 6.7 collective-permute-start.36
  487.7 5.6 collective-permute-start.37
  493.3 6.4 collective-permute-start.38
  494.8 7.4 collective-permute-start.39
  536.5 9.1 %collective-permute-start.42 = (f32[2,1,16,128]{3,2,1,0:T(8,128)S(1)}, f32[2,1,16,128]{3,2,1,0:T(8,128)S(1)}, u32[]{:S(2)}, u32[]{:S(2)}) collective-permute-start(f32[2,1,16,128]{3,2,1,0:T(8,128)S(1)} %get-tuple-element.1775), channel_id=1, source_target_pairs={{0,8},{8,16},{16,24},{1,9},{9,17},{17,25},{2,10},{10,18},{18,26},{... | collective-permute-start | bytes 49160 | tf_op jit(solution)/shard_map/ppermute | solution.py:29
  540.3 5.6 collective-permute-start.43
  547.8 7.4 collective-permute-start.45
  555.3 6.3 collective-permute-start.46
  600.1 8.3 %collective-permute-start.50 = (f32[2,6,1,128]{3,2,1,0:T(1,128)S(1)}, f32[2,6,1,128]{3,2,1,0:T(1,128)S(1)}, u32[]{:S(2)}, u32[]{:S(2)}) collective-permute-start(f32[2,6,1,128]{3,2,1,0:T(1,128)S(1)} %get-tuple-element.1755), channel_id=1, source_target_pairs={{0,2},{2,4},{4,6},{1,3},{3,5},{5,7},{8,10},{10,12},{12,14},{9,11},... | collective-permute-start | bytes 18440 | tf_op jit(solution)/shard_map/ppermute | solution.py:29
  603.4 7.5 collective-permute-start.51
  645.9 8.2 %collective-permute-start.54 = (f32[2,1,16,128]{3,2,1,0:T(8,128)S(1)}, f32[2,1,16,128]{3,2,1,0:T(8,128)S(1)}, u32[]{:S(2)}, u32[]{:S(2)}) collective-permute-start(f32[2,1,16,128]{3,2,1,0:T(8,128)S(1)} %get-tuple-element.1771), channel_id=1, source_target_pairs={{0,8},{8,16},{16,24},{1,9},{9,17},{17,25},{2,10},{10,18},{18,26},{... | collective-permute-start | bytes 49160 | tf_op jit(solution)/shard_map/ppermute | solution.py:29
  649.2 5.6 collective-permute-start.55
  656.7 7.4 collective-permute-start.57
  664.2 6.3 collective-permute-start.58
  (62 other events, 2063.2 us)
